TPU v7x, 32 devices: a whole 2x2x4 slice. The times are simulated.
32 devices in a mesh: dp: 8 (over z, y), expert: 4 (over x, core).
Axes of the slice: x: 2, y: 2, z: 4, core: 2. Of those that a mesh axis runs over, the one named last changes fastest.
Arguments:
- tokens: bfloat16 [1024, 4096], P('dp'), may hold values from -6 to 6
- expert_ids: int32 [1024, 2], P('dp'), may hold values from 0 to 3, all different within a row; in each aligned block of 128 rows (0 to 127, 128 to 255, ...) at most 96 rows name the same one
- gate_weights: float32 [1024, 2], P('dp'), may hold values from 0.2 to 1
- live_counts: int32 [8], P('dp'), may hold values from 64 to 128, as said below
- w_gate: bfloat16 [4, 4096, 8192], P('expert', None, 'dp'), may hold values from -0.09375 to 0.09375
- w_up: bfloat16 [4, 4096, 8192], P('expert', None, 'dp'), may hold values from -0.09375 to 0.09375
- w_down: bfloat16 [4, 8192, 4096], P('expert', 'dp'), may hold values from -0.0625 to 0.0625
Outputs:
- mixed: bfloat16 [1024, 4096], P('dp')
- total_loads: int32 [4], replicated
Inputs may be any that keep to these rules, and one draw needn't show every extreme that they name: `expert_ids`: each token names two different experts. Among the tokens of one rank no expert is named more than 96 times, a bound that some block reaches in some ranks. Rank r's first live_counts[r] tokens are live, the rest are padding. Some rank has all 128 tokens live.
All inputs are finite; a program needn't handle non-finite values.
Results may differ from a plain program's by a relative error of at most 0.017.
Values may be sent and summed in bfloat16 or wider, within the bound.
A program may use at most 128 MiB of HBM per device.

v0:
```python
import jax
import jax.numpy as jnp
from jax import lax
from jax.sharding import PartitionSpec as P


def plan_routes(expert_ids, live_total, n_experts, capacity):
    row_count = expert_ids.shape[0]
    is_live = jnp.arange(row_count, dtype=jnp.int32) < live_total
    flat_ids = expert_ids.reshape(-1)
    live_pairs = jnp.repeat(is_live, 2)
    one_hot = (
        (flat_ids[:, None] == jnp.arange(n_experts, dtype=jnp.int32)[None, :]) & live_pairs[:, None]
    ).astype(jnp.int32)
    earlier = jnp.cumsum(one_hot, axis=0) - one_hot
    slot_index = jnp.sum(earlier * one_hot, axis=1)
    targets = jnp.where(live_pairs, flat_ids * capacity + slot_index, -1)
    return (targets.reshape(row_count, 2), jnp.sum(one_hot, axis=0))


def dispatch_rows(tokens, targets, slots_all):
    wanted = targets.reshape(-1)[None, :] == jnp.arange(slots_all, dtype=jnp.int32)[:, None]
    wanted = jnp.any(wanted.reshape(slots_all, -1, 2), axis=2).astype(jnp.bfloat16)
    return jnp.dot(wanted, tokens, preferred_element_type=jnp.float32).astype(jnp.bfloat16)


def per_device(tokens, expert_ids, gate_weights, live_counts, w_gate, w_up, w_down):
    n_experts = lax.axis_size("expert")
    my_expert = lax.axis_index("expert")
    capacity = 3 * tokens.shape[0] // 4
    targets, expert_loads = plan_routes(expert_ids, live_counts[0], n_experts, capacity)
    local_slots = targets - my_expert * capacity
    outbound = dispatch_rows(tokens, local_slots, capacity)
    gathered = lax.all_gather(outbound, "dp", axis=0, tiled=True)
    gate_matrix = w_gate[0]
    up_matrix = w_up[0]
    down_matrix = w_down[0]
    gate_act = jnp.dot(gathered, gate_matrix, preferred_element_type=jnp.float32)
    up_act = jnp.dot(gathered, up_matrix, preferred_element_type=jnp.float32)
    hidden = (jax.nn.silu(gate_act) * up_act).astype(jnp.bfloat16)
    summed = lax.psum_scatter(
        jnp.dot(hidden, down_matrix, preferred_element_type=jnp.float32).astype(jnp.bfloat16),
        "dp",
        scatter_dimension=0,
        tiled=True,
    )
    is_mine = (local_slots >= 0) & (local_slots < capacity)
    pick_index = jnp.where(is_mine, local_slots, 0)
    selected = summed[pick_index].astype(jnp.float32)
    weights = jnp.where(is_mine, gate_weights, jnp.zeros_like(gate_weights))
    weighted = jnp.sum(weights[:, :, None] * selected, axis=1)
    mixed = lax.psum(weighted.astype(jnp.bfloat16), "expert")
    total_loads = lax.psum(expert_loads, "dp")
    return (mixed, total_loads)


def solution(mesh):
    placed = (
        P("dp", None),
        P("dp", None),
        P("dp", None),
        P("dp"),
        P("expert", None, "dp"),
        P("expert", None, "dp"),
        P("expert", "dp", None),
    )
    return jax.shard_map(
        per_device, mesh=mesh, in_specs=placed, out_specs=(P("dp", None), P()), check_vma=False
    )
```

profile of v0, /device:TPU:11, one launch (start us, length us, event | category | flops | bytes accessed | tf_op | source)
XLA Modules:
  0.0 328.0 jit_solution(15335059778489133544)
XLA Ops:
  7.2 0.8 broadcast_multiply_fusion
  8.0 0.8 copy.21
  8.8 0.1 eq.43
  8.9 0.1 eq.39
  9.7 0.1 broadcast_in_dim.23
  9.8 0.1 broadcast_in_dim.24
  10.0 0.1 broadcast_in_dim.22
  10.1 0.1 and.20
  10.2 0.1 copy.25
  10.3 1.2 reduce-window.6
  11.6 0.1 slice.10
  11.6 0.1 copy.23
  11.8 0.1 copy.24
  11.9 0.1 add_bitcast_fusion
  12.0 0.1 convert_reduce_fusion
  12.1 0.1 reduce_sum.30
  12.2 0.8 copy.26
  13.0 0.1 fusion.14
  13.1 0.1 copy.27
  13.2 1.2 convolution_convert_fusion
  14.5 97.3 %all-gather.2.cloned.1.call-done = bf16[768,4096]{1,0:T(8,128)(2,1)} async-done(((bf16[96,4096]{1,0:T(8,128)(2,1)}), bf16[768,4096]{1,0:T(8,128)(2,1)}) %all-gather.2.cloned.1.call-update) | async-done | bytes 6291472 | tf_op jit(solution)/shard_map/all_gather | solution.py:34
  111.9 12.1 %fusion.2 = f32[768,1024]{1,0:T(8,128)} fusion(bf16[768,4096]{1,0:T(8,128)(2,1)} %all-gather.2.cloned.1.call-done, bf16[1,4096,1024]{2,1,0:T(8,128)(2,1)} %param.12), kind=kOutput, calls=%fused_computation.3 | convolution fusion | flops 6442450944 | bytes 17825792 | tf_op jit(solution)/shard_map/dot_general | solution.py:39
  123.9 22.5 %fusion.6 = bf16[768,4096]{1,0:T(8,128)(2,1)} fusion(bf16[1,1024,4096]{2,1,0:T(8,128)(2,1)} %param.13, f32[768,1024]{1,0:T(8,128)} %fusion.2, bf16[768,4096]{1,0:T(8,128)(2,1)} %all-gather.2.cloned.1.call-done, bf16[1,4096,1024]{2,1,0:T(8,128)(2,1)} %param.11), kind=kOutput, calls=%fused_computation.7 | convolution fusion | flops 12892766208 | bytes 32505856 | tf_op jit(solution)/shard_map/dot_general | solution.py:42
  146.4 0.2 all-reduce.2.cloned.1.call-start
  146.7 0.1 reshape.48
  146.8 117.6 %reduce-scatter.2.cloned.1.call-done = bf16[96,4096]{1,0:T(8,128)(2,1)} async-done(((bf16[768,4096]{1,0:T(8,128)(2,1)}), bf16[96,4096]{1,0:T(8,128)(2,1)}) %reduce-scatter.2.cloned.1.call-update) | async-done | bytes 786448 | tf_op jit(solution)/shard_map/reduce_scatter | solution.py:41
  264.4 5.1 %gather_fusion = bf16[256,4096]{1,0:T(8,128)(2,1)S(1)} fusion(bf16[96,4096]{1,0:T(8,128)(2,1)} %reduce-scatter.2.cloned.1.call-done, s32[1024]{0:T(1024)S(1)} %pad_clamp_fusion), kind=kCustom, calls=%fused_computation | custom fusion | bytes 4195328 | tf_op jit(solution)/shard_map/gather | solution.py:49
  269.6 4.0 %reshape.56 = f32[128,2,4096]{2,1,0:T(2,128)} reshape(bf16[256,4096]{1,0:T(8,128)(2,1)S(1)} %gather_fusion) | data formatting | bytes 6291456 | tf_op jit(solution)/shard_map/convert_element_type | solution.py:49
  273.6 9.6 %multiply_reduce_fusion = bf16[128,4096]{1,0:T(8,128)(2,1)} fusion(f32[128,2,4096]{2,1,0:T(2,128)} %reshape.56, f32[128,2]{1,0:T(8,128)S(1)} %get-tuple-element.4), kind=kLoop, calls=%fused_computation.9 | loop fusion | flops 1572864 | bytes 5243904 | tf_op jit(solution)/shard_map/reduce_sum | solution.py:51
  283.2 8.2 %psum.15 = s32[4]{0:T(128)} all-reduce(s32[4]{0:T(128)S(1)} %get-tuple-element.2), channel_id=1, replica_groups=mesh['dp'=8,'expert'=4] {'dp'}, use_global_device_ids=true, to_apply=%region_8.9 | all-reduce | flops 4 | bytes 32 | tf_op jit(solution)/shard_map/psum | solution.py:53
  291.4 27.8 %all-reduce.2.cloned.1.call-done = bf16[128,4096]{1,0:T(8,128)(2,1)} async-done(((bf16[128,4096]{1,0:T(8,128)(2,1)}), bf16[128,4096]{1,0:T(8,128)(2,1)}) %all-reduce.2.cloned.1.call-update) | async-done | bytes 1048592 | tf_op jit(solution)/shard_map/psum | solution.py:52
  319.2 2.3 copy.33
  (15 shorter events, 0.3 us)
Async XLA Ops:
  7.2 6.1 %copy-start = (bf16[128,4096]{1,0:T(8,128)(2,1)S(1)}, bf16[128,4096]{1,0:T(8,128)(2,1)}, u32[]{:S(2)}) copy-start(bf16[128,4096]{1,0:T(8,128)(2,1)} %param.7) | copy-start | bytes 3145732
  7.2 104.7 %all-gather.2.cloned.1.call-start = ((), (), s32[]{:S(2)}) async-start(), calls=%async_computation.1 | async-start | bytes 7077888 | tf_op jit(solution)/shard_map/all_gather | solution.py:34
  14.5 249.9 %reduce-scatter.2.cloned.1.call-start = ((), (), s32[]{:S(2)}) async-start(), calls=%async_computation.2 | async-start | bytes 7077888 | tf_op jit(solution)/shard_map/reduce_scatter | solution.py:41
  146.4 172.8 %all-reduce.2.cloned.1.call-start = ((), (), s32[]{:S(2)}) async-start(), calls=%async_computation.3 | async-start | bytes 2097152 | tf_op jit(solution)/shard_map/psum | solution.py:52
Sparse Core Ops, SparseCore 0:
  14.6 97.2 all-gather.1
  146.5 117.8 reduce-scatter.1
  283.3 35.8 all-reduce.1
where the time goes:
time: 331 us; the launch traced here: 328 us
  waiting for transfers between devices  243 us (73%)
  matrix products  35.8 us (11%)
  between operations  14.5 us (4%)
  local copies, waits for them, and re-layouts  14.4 us (4%)
  other arithmetic  12 us (4%)
  blocking collectives  8.22 us (2%)
    reduce_scatter x1, waiting for transfers between devices, per_device(): lax.psum_scatter(jnp.dot(hidden, down_matrix, preferred_element_type=jnp....  118 us
    all_gather x1, waiting for transfers between devices, per_device(): gathered = lax.all_gather(outbound, 'dp', axis=0, tiled=True)  97.3 us
    psum x1, waiting for transfers between devices, per_device(): mixed = lax.psum(weighted.astype(jnp.bfloat16), 'expert')  27.8 us
    dot_general x1, matrix products, per_device(): jnp.dot(hidden, down_matrix, preferred_element_type=jnp.float32)  22.5 us
    dot_general x1, matrix products, per_device(): up_act = jnp.dot(gathered, up_matrix, preferred_element_type=jnp.float32)  12.1 us
    reduce_sum x1, other arithmetic, per_device(): weighted = jnp.sum(weights[:, :, None] * selected, axis=1)  9.64 us
    psum x1, blocking collectives, per_device(): total_loads = lax.psum(expert_loads, 'dp')  8.22 us
  transfers between devices with their start and end apart: 3, of which 3 were waited for; matrix products, arithmetic and copies ran while one was open for 0% of the time, Pallas kernels for 0%

commit v1 on v0

v1 whole, which is shorter than its diff:
```python
import functools

import jax
import jax.numpy as jnp
from jax import lax
from jax.experimental import pallas as pl
from jax.experimental.pallas import tpu as pltpu
from jax.sharding import PartitionSpec as P

MESH = pl.DeviceIdType.MESH
BF16, F32 = jnp.bfloat16, jnp.float32


def routing_weights(expert_ids, gate_weights, live_total, n_experts, my_expert):
    live = (jnp.arange(expert_ids.shape[0], dtype=jnp.int32) < live_total)[:, None]
    mine = (expert_ids == my_expert) & live
    weight = jnp.sum(jnp.where(mine, gate_weights, 0.0), axis=1)
    named = (expert_ids[:, :, None] == jnp.arange(n_experts, dtype=jnp.int32)) & live[:, :, None]
    return weight, jnp.sum(named.astype(jnp.int32), axis=(0, 1))


def general(tokens, expert_ids, gate_weights, live_counts, w_gate, w_up, w_down):
    weight, loads = routing_weights(
        expert_ids, gate_weights, live_counts[0], lax.axis_size("expert"), lax.axis_index("expert")
    )
    rows = lax.all_gather(tokens, "dp", axis=0, tiled=True)
    scale = lax.all_gather(weight, "dp", axis=0, tiled=True)[:, None]
    gate_act = jnp.dot(rows, w_gate[0], preferred_element_type=F32)
    up_act = jnp.dot(rows, w_up[0], preferred_element_type=F32)
    hidden = (jax.nn.silu(gate_act) * up_act * scale).astype(BF16)
    partial = jnp.dot(hidden, w_down[0], preferred_element_type=F32).astype(BF16)
    summed = lax.psum_scatter(partial, "dp", scatter_dimension=0, tiled=True)
    return lax.psum(summed, "expert"), lax.psum(loads, "dp")


def kernel(n_y, n_planes, tokens, meta, w_gate, w_up, w_down, out, meta_out,
           G, M, WG, WU, WD, H, Y, RC, RY0, RX0, RX1, RY1, RZ, OUT, send_sem, recv_sem, local_sem):
    dp, ex = lax.axis_index("dp"), lax.axis_index("expert")
    z, y = dp // n_y, dp % n_y
    x, c = ex // 2, ex % 2
    yo, xo, co = 1 - y, 1 - x, 1 - c
    n_dp = n_y * n_planes
    pieces, rows, width = G.shape[1:]
    half, quarter = pieces // 2, pieces // 4

    def xor(a, k):
        lo, hi = a % 2, a // 2
        lo = lo if k % 2 == 0 else 1 - lo
        hi = hi if k // 2 == 0 else hi + 1 - 2 * (hi % 2)
        return hi * 2 + lo

    plane = [xor(z, k) for k in range(n_planes)]
    y_peer, x_peer, core_peer = (z * n_y + yo, ex), (dp, xo * 2 + c), (dp, x * 2 + co)
    z_peer = [(plane[k] * n_y + y, ex) for k in range(n_planes)]
    me = dp
    rank = [plane[k] * n_y + y for k in range(n_planes)]
    other = [plane[k] * n_y + yo for k in range(n_planes)]
    pair = [pl.ds(plane[k] * n_y, n_y) for k in range(n_planes)]

    peers = [(lax.rem(dp + d, n_dp), ex) for d in range(1, n_dp)] + [x_peer, core_peer]
    barrier = pltpu.get_barrier_semaphore()

    n_local = [0]

    def local(src, dst):
        copy = pltpu.make_async_copy(src, dst, local_sem.at[n_local[0]])
        n_local[0] += 1
        copy.start()
        return copy

    own_loads = [local(tokens.at[:, pl.ds(q * width, width)], G.at[me, q]) for q in range(pieces)]
    own_meta = local(meta, M.at[me])
    weight_loads = [local(w_gate.at[0], WG), local(w_up.at[0], WU), local(w_down.at[0], WD)]

    for a, b in peers:
        pl.semaphore_signal(barrier, inc=1, device_id={"dp": a, "expert": b}, device_id_type=MESH)
    pl.semaphore_wait(barrier, len(peers))

    sent = []

    def send(src, dst, to):
        i = len(sent)
        copy = pltpu.make_async_remote_copy(
            src_ref=src, dst_ref=dst, send_sem=send_sem.at[i], recv_sem=recv_sem.at[i],
            device_id={"dp": to[0], "expert": to[1]}, device_id_type=MESH,
        )
        copy.start()
        sent.append(copy)
        return copy

    def got(*copies):
        for copy in copies:
            copy.wait_recv()

    mine_x = pl.ds(c * half + x * quarter, quarter)
    mine_c, other_c = pl.ds(c * half, half), pl.ds(co * half, half)

    def piece(xh, o):
        return c * half + xh * quarter + o

    for copy in own_loads:
        copy.wait()
    own_meta.wait()

    ZS = [None] + [send(G.at[me, mine_x], G.at[me, mine_x], z_peer[k]) for k in range(1, n_planes)]
    A0 = send(G.at[me, mine_x], G.at[me, mine_x], y_peer)
    metas = [send(M.at[me], M.at[me], (lax.rem(dp + d, n_dp), ex)) for d in range(1, n_dp)]

    def stage_a(k):
        got(ZS[k])
        ref = G.at[rank[k], piece(x, 0)]
        ref1 = G.at[rank[k], piece(x, 1)]
        return send(ref, ref, x_peer), send(ref1, ref1, y_peer)

    def stage_b(k, a):
        got(a[0])
        first = [G.at[rank[k], piece(h, 0)] for h in range(2)]
        b = [send(ref, ref, y_peer) for ref in first]
        got(a[1])
        ref = G.at[pair[k], piece(x, 1)]
        return b + [send(ref, ref, x_peer)]

    def stage_d(k, b):
        got(*b)
        ref = G.at[pair[k], mine_c]
        return send(ref, ref, core_peer)

    h_tile = min(256, WG.shape[1])

    def gate_up(k):
        columns = [jnp.transpose(M[plane[k] * n_y + j])[:, 0:1] for j in range(n_y)]
        scale = jnp.concatenate(columns, axis=0)

        def tile(t, carry):
            cols = pl.ds(pl.multiple_of(t * h_tile, h_tile), h_tile)
            g = jnp.zeros((n_y * rows, h_tile), F32)
            u = jnp.zeros((n_y * rows, h_tile), F32)
            for q in range(pieces):
                block = G[pair[k], q].reshape(n_y * rows, width)
                g += jnp.dot(block, WG[q * width:(q + 1) * width, cols], preferred_element_type=F32)
            for q in range(pieces):
                block = G[pair[k], q].reshape(n_y * rows, width)
                u += jnp.dot(block, WU[q * width:(q + 1) * width, cols], preferred_element_type=F32)
            H[k, :, cols] = (g / (1.0 + jnp.exp(-g)) * u * scale).astype(BF16)
            return carry

        lax.fori_loop(0, WG.shape[1] // h_tile, tile, 0)

    def down(k):
        def tile(q, carry):
            cols = pl.ds(pl.multiple_of(q * width, width), width)
            part = jnp.dot(H[k], WD[:, cols], preferred_element_type=F32).astype(BF16)
            Y[pair[k], q] = part.reshape(n_y, rows, width)
            return carry

        lax.fori_loop(0, pieces, tile, 0)
        return send(Y.at[pair[k], other_c], RC.at[k], core_peer)

    def add(r, q, value):
        Y[r, q] = (Y[r, q].astype(F32) + value.astype(F32)).astype(BF16)

    def reduce_1(k, r0):
        got(r0)
        for j in range(n_y):
            def tile(q, carry):
                add(plane[k] * n_y + j, c * half + q, RC[k, j, q])
                return carry
            lax.fori_loop(0, half, tile, 0)
        to_y = [send(Y.at[other[k], piece(h, 0)], RY0.at[k, h], y_peer) for h in range(2)]
        to_x = send(Y.at[pair[k], piece(xo, 1)], RX1.at[k], x_peer)
        return to_y, to_x

    def reduce_2(k, r1):
        to_y, to_x = r1
        got(*to_y)
        for h in range(2):
            add(rank[k], piece(h, 0), RY0[k, h])
        x0 = send(Y.at[rank[k], piece(xo, 0)], RX0.at[k], x_peer)
        got(to_x)
        for j in range(n_y):
            add(plane[k] * n_y + j, piece(x, 1), RX1[k, j])
        y1 = send(Y.at[other[k], piece(x, 1)], RY1.at[k], y_peer)
        return x0, y1

    def reduce_3(k, r2):
        got(r2[0])
        add(rank[k], piece(x, 0), RX0[k])
        got(r2[1])
        add(rank[k], piece(x, 1), RY1[k])
        if k:
            return send(Y.at[rank[k], mine_x], RZ.at[k - 1], z_peer[k])

    got(A0)
    ref = G.at[other[0], mine_x]
    B0 = send(ref, ref, x_peer)
    A1 = stage_a(1)
    got(B0)
    ref = G.at[other[0], mine_c]
    D0 = send(ref, ref, core_peer)
    B1 = stage_b(1, A1)
    got(D0)
    got(*metas)
    weight_loads[0].wait()
    weight_loads[1].wait()
    gate_up(0)
    A2 = stage_a(2)
    B2 = stage_b(2, A2)
    D1 = stage_d(1, B1)
    A3 = stage_a(3)
    got(D1)
    gate_up(1)
    B3 = stage_b(3, A3)
    D2 = stage_d(2, B2)
    weight_loads[2].wait()
    C1 = down(1)
    got(D2)
    gate_up(2)
    D3 = stage_d(3, B3)
    P1 = reduce_1(1, C1)
    C2 = down(2)
    got(D3)
    gate_up(3)
    P2 = reduce_1(2, C2)
    Q1 = reduce_2(1, P1)
    C3 = down(3)
    C0 = down(0)
    P3 = reduce_1(3, C3)
    F1 = reduce_3(1, Q1)
    Q2 = reduce_2(2, P2)
    P0 = reduce_1(0, C0)
    F2 = reduce_3(2, Q2)
    Q3 = reduce_2(3, P3)
    F3 = reduce_3(3, Q3)
    Q0 = reduce_2(0, P0)
    reduce_3(0, Q0)

    total = M[0]
    for r in range(1, n_dp):
        total = total + M[r]
    meta_out[...] = total

    got(F1, F2, F3)
    to_x = []
    for o in range(quarter):
        value = Y[me, piece(x, o)].astype(F32)
        for k in range(n_planes - 1):
            value = value + RZ[k, o].astype(F32)
        OUT[piece(x, o)] = value.astype(BF16)
        ref = OUT.at[piece(x, o)]
        to_x.append((send(ref, ref, x_peer), send(ref, ref, core_peer)))
    stores = []

    def store(q):
        stores.append(local(OUT.at[q], out.at[:, pl.ds(pl.multiple_of(q * width, width), width)]))

    last = []
    for o in range(quarter):
        store(piece(x, o))
        got(to_x[o][0])
        ref = OUT.at[piece(xo, o)]
        last.append(send(ref, ref, core_peer))
        store(piece(xo, o))
    for o in range(quarter):
        got(to_x[o][1])
        store(co * half + x * quarter + o)
    for o in range(quarter):
        got(last[o])
        store(co * half + xo * quarter + o)
    for copy in stores:
        copy.wait()
    for copy in sent:
        copy.wait_send()


def planned(n_y, n_planes, tokens, expert_ids, gate_weights, live_counts, w_gate, w_up, w_down):
    n_experts = lax.axis_size("expert")
    rows, model = tokens.shape
    hidden = w_gate.shape[2]
    n_dp, pieces = n_y * n_planes, 8
    width, half, quarter = model // pieces, pieces // 2, pieces // 4
    weight, loads = routing_weights(
        expert_ids, gate_weights, live_counts[0], n_experts, lax.axis_index("expert")
    )
    line = jnp.zeros((rows,), F32).at[:n_experts].set(loads.astype(F32))
    meta = jnp.concatenate([weight[None], line[None], jnp.zeros((6, rows), F32)], axis=0)
    hbm = pl.BlockSpec(memory_space=pl.ANY)
    vmem = pl.BlockSpec(memory_space=pltpu.VMEM)
    mixed, totals = pl.pallas_call(
        functools.partial(kernel, n_y, n_planes),
        name="moe",
        out_shape=(jax.ShapeDtypeStruct((rows, model), BF16), jax.ShapeDtypeStruct((8, rows), F32)),
        in_specs=[hbm] * 5,
        out_specs=(hbm, vmem),
        scratch_shapes=[
            pltpu.VMEM((n_dp, pieces, rows, width), BF16),
            pltpu.VMEM((n_dp, 8, rows), F32),
            pltpu.VMEM((model, hidden), BF16),
            pltpu.VMEM((model, hidden), BF16),
            pltpu.VMEM((hidden, model), BF16),
            pltpu.VMEM((n_planes, n_y * rows, hidden), BF16),
            pltpu.VMEM((n_dp, pieces, rows, width), BF16),
            pltpu.VMEM((n_planes, n_y, half, rows, width), BF16),
            pltpu.VMEM((n_planes, 2, rows, width), BF16),
            pltpu.VMEM((n_planes, rows, width), BF16),
            pltpu.VMEM((n_planes, n_y, rows, width), BF16),
            pltpu.VMEM((n_planes, rows, width), BF16),
            pltpu.VMEM((n_planes - 1, quarter, rows, width), BF16),
            pltpu.VMEM((pieces, rows, width), BF16),
            pltpu.SemaphoreType.DMA((96,)),
            pltpu.SemaphoreType.DMA((96,)),
            pltpu.SemaphoreType.DMA((32,)),
        ],
        compiler_params=pltpu.CompilerParams(
            collective_id=0, has_side_effects=True, vmem_limit_bytes=63 * 2**20
        ),
    )(tokens, meta, w_gate, w_up, w_down)
    return mixed, totals[1, :n_experts].astype(jnp.int32)


def solution(mesh):
    n_dp, n_experts = mesh.shape["dp"], mesh.shape["expert"]
    n_x = n_experts // 2
    n_y = n_x
    n_planes = n_dp // n_y
    body = general
    if n_y == 2 and n_planes == 4:
        body = functools.partial(planned, n_y, n_planes)
    placed = (
        P("dp", None),
        P("dp", None),
        P("dp", None),
        P("dp"),
        P("expert", None, "dp"),
        P("expert", None, "dp"),
        P("expert", "dp", None),
    )
    return jax.shard_map(
        body, mesh=mesh, in_specs=placed, out_specs=(P("dp", None), P()), check_vma=False
    )
```

time: 331 us -> 127 us (0.38)
  waiting for transfers between devices: 243 us -> 0 us
  Pallas kernels: 0 us -> 120 us
  matrix products: 35.8 us -> 0 us
  between operations: 14.5 us -> 1.3 us
  local copies, waits for them, and re-layouts: 14.4 us -> 2.36 us
  other arithmetic: 12 us -> 3.38 us
  blocking collectives: 8.22 us -> 0 us
    pallas_call x0 -> x1, Pallas kernels: none -> 120 us  [planned(): pl.pallas_call(functools.partial(kernel, n_y, n_planes), name='moe', out_...]
    reduce_scatter x1 -> x0, waiting for transfers between devices: 118 us -> none  [per_device(): lax.psum_scatter(jnp.dot(hidden, down_matrix, preferred_element_type=jnp....]
    all_gather x1 -> x0, waiting for transfers between devices: 97.3 us -> none  [per_device(): gathered = lax.all_gather(outbound, 'dp', axis=0, tiled=True)]
    dot_general x3 -> x0, matrix products: 35.8 us -> none  [the longest x1 22.5 us: per_device(): jnp.dot(hidden, down_matrix, preferred_element_type=jnp.float32)]
    psum x1 -> x0, waiting for transfers between devices: 27.8 us -> none  [per_device(): mixed = lax.psum(weighted.astype(jnp.bfloat16), 'expert')]
    reduce_sum x2, other arithmetic: 9.76 us -> 1.51 us  [the longest x1 0.8 us: routing_weights(): return (weight, jnp.sum(named.astype(jnp.int32), axis=(0, 1)))]
    psum x1 -> x0, blocking collectives: 8.22 us -> none  [per_device(): total_loads = lax.psum(expert_loads, 'dp')]
    gather x1 -> x0, local copies, waits for them, and re-layouts: 5.12 us -> none  [per_device(): selected = summed[pick_index].astype(jnp.float32)]
  transfers between devices with their start and end apart: 3 -> 0, of which waited for: 3 -> 0; matrix products, arithmetic and copies ran while one was open for 0% -> 0% of each run, Pallas kernels for 0% -> 0%
where the time goes in v1:
time: 127 us
  Pallas kernels  120 us (94%)
  other arithmetic  3.38 us (3%)
  local copies, waits for them, and re-layouts  2.36 us (2%)
  between operations  1.3 us (1%)
    pallas_call x1, Pallas kernels, planned(): pl.pallas_call(functools.partial(kernel, n_y, n_planes), name='moe', out_...  120 us

profile of v1, /device:TPU:11, one launch (start us, length us, event | category | flops | bytes accessed | tf_op | source)
XLA Modules:
  0.0 126.9 jit_solution(13861653436789254553)
XLA Ops:
  1.3 0.7 fusion.3
  2.0 0.8 convert_reduce_fusion
  2.8 0.1 pad.5.clone
  2.9 0.7 fusion.meta
  3.6 119.8 %moe.1 = (bf16[128,4096]{1,0:T(8,128)(2,1)}, f32[8,128]{1,0:T(8,128)}) custom-call(bf16[128,4096]{1,0:T(8,128)(2,1)} %tokens.1, f32[8,128]{1,0:T(8,128)} %fusion.meta, bf16[1,4096,1024]{2,1,0:T(8,128)(2,1)} %w_gate.1, bf16[1,4096,1024]{2,1,0:T(8,128)(2,1)} %w_up.1, bf16[1,1024,4096]{2,1,0:T(8,128)(2,1)} %w_down.1), custom_call_target="tpu_custom_call" | custom-call | tf_op jit(solution)/shard_map/moe/pallas_call | solution.py:288
  123.4 1.2 convert_bitcast_fusion
  124.6 2.3 %copy.12 = bf16[128,4096]{1,0:T(8,128)(2,1)} copy(bf16[128,4096]{1,0:T(8,128)(2,1)} %get-tuple-element.20) | data formatting | bytes 2097152
  (3 shorter events, 0.0 us)

commit v2 on v1

--- a/solution.py
+++ b/solution.py
@@ -9,6 +9,9 @@
 
 MESH = pl.DeviceIdType.MESH
 BF16, F32 = jnp.bfloat16, jnp.float32
+
+
+ORDER = "B0 A1 B1 D0 A2 D1 B2 g1 A3 h1 g0 D2 d1 B3 g2 P1 h2 d2 D3 P2 g3 Q1 h3 d3 Q2 F1 P3 F2 h0 d0 Q3 P0 F3 Q0 F0"
 
 
 def routing_weights(expert_ids, gate_weights, live_total, n_experts, my_expert):
@@ -102,32 +105,53 @@
         copy.wait()
     own_meta.wait()
 
-    ZS = [None] + [send(G.at[me, mine_x], G.at[me, mine_x], z_peer[k]) for k in range(1, n_planes)]
-    A0 = send(G.at[me, mine_x], G.at[me, mine_x], y_peer)
+    own = [G.at[me, piece(x, o)] for o in range(quarter)]
+    A = {0: [send(ref, ref, y_peer) for ref in own]}
+    ZS = {k: [send(ref, ref, z_peer[k]) for ref in own] for k in range(1, n_planes)}
     metas = [send(M.at[me], M.at[me], (lax.rem(dp + d, n_dp), ex)) for d in range(1, n_dp)]
 
+    B, D, C, R1, R2, F = {}, {}, {}, {}, {}, {}
+
     def stage_a(k):
-        got(ZS[k])
-        ref = G.at[rank[k], piece(x, 0)]
-        ref1 = G.at[rank[k], piece(x, 1)]
-        return send(ref, ref, x_peer), send(ref1, ref1, y_peer)
-
-    def stage_b(k, a):
-        got(a[0])
-        first = [G.at[rank[k], piece(h, 0)] for h in range(2)]
-        b = [send(ref, ref, y_peer) for ref in first]
-        got(a[1])
+        sends = []
+        for o, to in ((0, x_peer), (1, y_peer)):
+            got(ZS[k][o])
+            ref = G.at[rank[k], piece(x, o)]
+            sends.append(send(ref, ref, to))
+        A[k] = sends
+
+    def stage_b(k):
+        B[k] = []
+        if k == 0:
+            for o in range(2):
+                got(A[0][o])
+                ref = G.at[other[0], piece(x, o)]
+                B[0].append(send(ref, ref, x_peer))
+            return
+        got(A[k][0])
+        for h in range(2):
+            ref = G.at[rank[k], piece(h, 0)]
+            B[k].append(send(ref, ref, y_peer))
+        got(A[k][1])
         ref = G.at[pair[k], piece(x, 1)]
-        return b + [send(ref, ref, x_peer)]
-
-    def stage_d(k, b):
-        got(*b)
-        ref = G.at[pair[k], mine_c]
-        return send(ref, ref, core_peer)
-
+        B[k].append(send(ref, ref, x_peer))
+
+    def stage_d(k):
+        got(*B[k])
+        ref = G.at[pair[k] if k else other[0], mine_c]
+        D[k] = send(ref, ref, core_peer)
+
+    any_done, down_done = [], []
     h_tile = min(256, WG.shape[1])
 
-    def gate_up(k):
+    def gate_up(k, part):
+        if part == 0:
+            got(D[k])
+            if not any_done:
+                any_done.append(k)
+                got(*metas)
+                weight_loads[0].wait()
+                weight_loads[1].wait()
         columns = [jnp.transpose(M[plane[k] * n_y + j])[:, 0:1] for j in range(n_y)]
         scale = jnp.concatenate(columns, axis=0)
 
@@ -144,9 +168,13 @@
             H[k, :, cols] = (g / (1.0 + jnp.exp(-g)) * u * scale).astype(BF16)
             return carry
 
-        lax.fori_loop(0, WG.shape[1] // h_tile, tile, 0)
+        steps = WG.shape[1] // h_tile // 2
+        lax.fori_loop(part * steps, (part + 1) * steps, tile, 0)
 
     def down(k):
+        if not down_done:
+            down_done.append(k)
+            weight_loads[2].wait()
         def tile(q, carry):
             cols = pl.ds(pl.multiple_of(q * width, width), width)
             part = jnp.dot(H[k], WD[:, cols], preferred_element_type=F32).astype(BF16)
@@ -154,13 +182,13 @@
             return carry
 
         lax.fori_loop(0, pieces, tile, 0)
-        return send(Y.at[pair[k], other_c], RC.at[k], core_peer)
+        C[k] = send(Y.at[pair[k], other_c], RC.at[k], core_peer)
 
     def add(r, q, value):
         Y[r, q] = (Y[r, q].astype(F32) + value.astype(F32)).astype(BF16)
 
-    def reduce_1(k, r0):
-        got(r0)
+    def reduce_1(k):
+        got(C[k])
         for j in range(n_y):
             def tile(q, carry):
                 add(plane[k] * n_y + j, c * half + q, RC[k, j, q])
@@ -168,10 +196,10 @@
             lax.fori_loop(0, half, tile, 0)
         to_y = [send(Y.at[other[k], piece(h, 0)], RY0.at[k, h], y_peer) for h in range(2)]
         to_x = send(Y.at[pair[k], piece(xo, 1)], RX1.at[k], x_peer)
-        return to_y, to_x
-
-    def reduce_2(k, r1):
-        to_y, to_x = r1
+        R1[k] = to_y, to_x
+
+    def reduce_2(k):
+        to_y, to_x = R1[k]
         got(*to_y)
         for h in range(2):
             add(rank[k], piece(h, 0), RY0[k, h])
@@ -180,66 +208,30 @@
         for j in range(n_y):
             add(plane[k] * n_y + j, piece(x, 1), RX1[k, j])
         y1 = send(Y.at[other[k], piece(x, 1)], RY1.at[k], y_peer)
-        return x0, y1
-
-    def reduce_3(k, r2):
+        R2[k] = x0, y1
+
+    def reduce_3(k):
+        r2 = R2[k]
         got(r2[0])
         add(rank[k], piece(x, 0), RX0[k])
         got(r2[1])
         add(rank[k], piece(x, 1), RY1[k])
         if k:
-            return send(Y.at[rank[k], mine_x], RZ.at[k - 1], z_peer[k])
-
-    got(A0)
-    ref = G.at[other[0], mine_x]
-    B0 = send(ref, ref, x_peer)
-    A1 = stage_a(1)
-    got(B0)
-    ref = G.at[other[0], mine_c]
-    D0 = send(ref, ref, core_peer)
-    B1 = stage_b(1, A1)
-    got(D0)
-    got(*metas)
-    weight_loads[0].wait()
-    weight_loads[1].wait()
-    gate_up(0)
-    A2 = stage_a(2)
-    B2 = stage_b(2, A2)
-    D1 = stage_d(1, B1)
-    A3 = stage_a(3)
-    got(D1)
-    gate_up(1)
-    B3 = stage_b(3, A3)
-    D2 = stage_d(2, B2)
-    weight_loads[2].wait()
-    C1 = down(1)
-    got(D2)
-    gate_up(2)
-    D3 = stage_d(3, B3)
-    P1 = reduce_1(1, C1)
-    C2 = down(2)
-    got(D3)
-    gate_up(3)
-    P2 = reduce_1(2, C2)
-    Q1 = reduce_2(1, P1)
-    C3 = down(3)
-    C0 = down(0)
-    P3 = reduce_1(3, C3)
-    F1 = reduce_3(1, Q1)
-    Q2 = reduce_2(2, P2)
-    P0 = reduce_1(0, C0)
-    F2 = reduce_3(2, Q2)
-    Q3 = reduce_2(3, P3)
-    F3 = reduce_3(3, Q3)
-    Q0 = reduce_2(0, P0)
-    reduce_3(0, Q0)
+            F[k] = send(Y.at[rank[k], mine_x], RZ.at[k - 1], z_peer[k])
+
+    units = {
+        "A": stage_a, "B": stage_b, "D": stage_d, "g": lambda k: gate_up(k, 0), "h": lambda k: gate_up(k, 1),
+        "d": down, "P": reduce_1, "Q": reduce_2, "F": reduce_3,
+    }
+    for unit in ORDER.split():
+        units[unit[0]](int(unit[1]))
 
     total = M[0]
     for r in range(1, n_dp):
         total = total + M[r]
     meta_out[...] = total
 
-    got(F1, F2, F3)
+    got(*F.values())
     to_x = []
     for o in range(quarter):
         value = Y[me, piece(x, o)].astype(F32)

time: 127 us -> 113 us (0.89); the launches traced: 127 us -> 111 us
  Pallas kernels: 120 us -> 104 us
    pallas_call x1, Pallas kernels: 120 us -> 104 us  [planned(): pl.pallas_call(functools.partial(kernel, n_y, n_planes), name='moe', out_...]
where the time goes in v2:
time: 113 us; the launch traced here: 111 us
  Pallas kernels  104 us (92%)
  other arithmetic  3.38 us (3%)
  local copies, waits for them, and re-layouts  2.36 us (2%)
  between operations  1.3 us (1%)
    pallas_call x1, Pallas kernels, planned(): pl.pallas_call(functools.partial(kernel, n_y, n_planes), name='moe', out_...  104 us
    unnamed x1, local copies, waits for them, and re-layouts  2.29 us

profile of v2, /device:TPU:11, one launch (start us, length us, event | category | flops | bytes accessed | tf_op | source)
XLA Modules:
  0.0 110.5 jit_solution(908013944146332186)
XLA Ops:
  1.3 0.7 fusion.3
  2.0 0.8 convert_reduce_fusion
  2.8 0.1 pad.5.clone
  2.9 0.7 fusion.meta
  3.6 103.5 %moe.1 = (bf16[128,4096]{1,0:T(8,128)(2,1)}, f32[8,128]{1,0:T(8,128)}) custom-call(bf16[128,4096]{1,0:T(8,128)(2,1)} %tokens.1, f32[8,128]{1,0:T(8,128)} %fusion.meta, bf16[1,4096,1024]{2,1,0:T(8,128)(2,1)} %w_gate.1, bf16[1,4096,1024]{2,1,0:T(8,128)(2,1)} %w_up.1, bf16[1,1024,4096]{2,1,0:T(8,128)(2,1)} %w_down.1), custom_call_target="tpu_custom_call" | custom-call | tf_op jit(solution)/shard_map/moe/pallas_call | solution.py:280
  107.1 1.2 %convert_bitcast_fusion = s32[4]{0:T(128)} fusion(f32[8,128]{1,0:T(8,128)} %get-tuple-element.17), kind=kLoop, calls=%fused_computation.10 | loop fusion | flops 4 | bytes 32 | tf_op jit(solution)/shard_map/convert_element_type | solution.py:309
  108.3 2.3 %copy.12 = bf16[128,4096]{1,0:T(8,128)(2,1)} copy(bf16[128,4096]{1,0:T(8,128)(2,1)} %get-tuple-element.20) | data formatting | bytes 2097152
  (3 shorter events, 0.0 us)

commit v3 on v2

--- a/solution.py
+++ b/solution.py
@@ -11,7 +11,7 @@
 BF16, F32 = jnp.bfloat16, jnp.float32
 
 
-ORDER = "B0 A1 B1 D0 A2 D1 B2 g1 A3 h1 g0 D2 d1 B3 g2 P1 h2 d2 D3 P2 g3 Q1 h3 d3 Q2 F1 P3 F2 h0 d0 Q3 P0 F3 Q0 F0"
+ORDER = "B0 A1 B1 D0 A2 D1 B2 g1 A3 h1 D2 d1 B3 g2 P1 h2 d2 D3 P2 g0 Q1 R1 g3 h3 d3 F1 Q2 R2 P3 h0 F2 d0 Q3 R3 P0 F3 X0 X1"
 
 
 def routing_weights(expert_ids, gate_weights, live_total, n_experts, my_expert):
@@ -37,7 +37,7 @@
 
 
 def kernel(n_y, n_planes, tokens, meta, w_gate, w_up, w_down, out, meta_out,
-           G, M, WG, WU, WD, H, Y, RC, RY0, RX0, RX1, RY1, RZ, OUT, send_sem, recv_sem, local_sem):
+           G, M, WG, WU, WD, H, Y, RC, RY0, RX0, RX1, RY1, RZ, RO, RP, OUT, send_sem, recv_sem, local_sem):
     dp, ex = lax.axis_index("dp"), lax.axis_index("expert")
     z, y = dp // n_y, dp % n_y
     x, c = ex // 2, ex % 2
@@ -141,6 +141,7 @@
         ref = G.at[pair[k] if k else other[0], mine_c]
         D[k] = send(ref, ref, core_peer)
 
+    OY, OX = [], []
     any_done, down_done = [], []
     h_tile = min(256, WG.shape[1])
 
@@ -181,7 +182,7 @@
             Y[pair[k], q] = part.reshape(n_y, rows, width)
             return carry
 
-        lax.fori_loop(0, pieces, tile, 0)
+        lax.fori_loop(0, pieces, tile, 0, unroll=2)
         C[k] = send(Y.at[pair[k], other_c], RC.at[k], core_peer)
 
     def add(r, q, value):
@@ -194,21 +195,40 @@
                 add(plane[k] * n_y + j, c * half + q, RC[k, j, q])
                 return carry
             lax.fori_loop(0, half, tile, 0)
+        if k == 0:
+            for xh in (xo, x):
+                for o in range(quarter):
+                    OY.append(send(Y.at[other[0], piece(xh, o)], RO.at[len(OY)], y_peer))
+            return
         to_y = [send(Y.at[other[k], piece(h, 0)], RY0.at[k, h], y_peer) for h in range(2)]
         to_x = send(Y.at[pair[k], piece(xo, 1)], RX1.at[k], x_peer)
         R1[k] = to_y, to_x
 
-    def reduce_2(k):
-        to_y, to_x = R1[k]
-        got(*to_y)
+    def reduce_2x(k):
+        got(*R1[k][0])
         for h in range(2):
             add(rank[k], piece(h, 0), RY0[k, h])
-        x0 = send(Y.at[rank[k], piece(xo, 0)], RX0.at[k], x_peer)
-        got(to_x)
+        R2[k] = [send(Y.at[rank[k], piece(xo, 0)], RX0.at[k], x_peer)]
+
+    def reduce_2y(k):
+        got(R1[k][1])
         for j in range(n_y):
             add(plane[k] * n_y + j, piece(x, 1), RX1[k, j])
-        y1 = send(Y.at[other[k], piece(x, 1)], RY1.at[k], y_peer)
-        R2[k] = x0, y1
+        R2[k].append(send(Y.at[other[k], piece(x, 1)], RY1.at[k], y_peer))
+
+    def own_x(half_sent):
+        xh = (xo, x)[half_sent]
+        if half_sent:
+            got(*F.values())
+        for o in range(quarter):
+            got(OY[half_sent * quarter + o])
+            value = Y[me, piece(xh, o)].astype(F32) + RO[half_sent * quarter + o].astype(F32)
+            if half_sent:
+                for k in range(n_planes - 1):
+                    value = value + RZ[k, o].astype(F32)
+            Y[me, piece(xh, o)] = value.astype(BF16)
+            src = Y.at[me, piece(xh, o)]
+            OX.append(send(src, RP.at[half_sent * quarter + o], x_peer))
 
     def reduce_3(k):
         r2 = R2[k]
@@ -216,12 +236,12 @@
         add(rank[k], piece(x, 0), RX0[k])
         got(r2[1])
         add(rank[k], piece(x, 1), RY1[k])
-        if k:
-            F[k] = send(Y.at[rank[k], mine_x], RZ.at[k - 1], z_peer[k])
+        F[k] = send(Y.at[rank[k], mine_x], RZ.at[k - 1], z_peer[k])
 
     units = {
         "A": stage_a, "B": stage_b, "D": stage_d, "g": lambda k: gate_up(k, 0), "h": lambda k: gate_up(k, 1),
-        "d": down, "P": reduce_1, "Q": reduce_2, "F": reduce_3,
+        "d": down, "P": reduce_1, "Q": reduce_2x, "R": reduce_2y, "F": reduce_3,
+        "X": own_x,
     }
     for unit in ORDER.split():
         units[unit[0]](int(unit[1]))
@@ -231,33 +251,25 @@
         total = total + M[r]
     meta_out[...] = total
 
-    got(*F.values())
-    to_x = []
-    for o in range(quarter):
-        value = Y[me, piece(x, o)].astype(F32)
-        for k in range(n_planes - 1):
-            value = value + RZ[k, o].astype(F32)
-        OUT[piece(x, o)] = value.astype(BF16)
-        ref = OUT.at[piece(x, o)]
-        to_x.append((send(ref, ref, x_peer), send(ref, ref, core_peer)))
-    stores = []
+    stores, last = [], []
 
     def store(q):
         stores.append(local(OUT.at[q], out.at[:, pl.ds(pl.multiple_of(q * width, width), width)]))
 
-    last = []
-    for o in range(quarter):
-        store(piece(x, o))
-        got(to_x[o][0])
-        ref = OUT.at[piece(xo, o)]
-        last.append(send(ref, ref, core_peer))
-        store(piece(xo, o))
-    for o in range(quarter):
-        got(to_x[o][1])
-        store(co * half + x * quarter + o)
-    for o in range(quarter):
-        got(last[o])
-        store(co * half + xo * quarter + o)
+    for i in range(2):
+        xh = (x, xo)[i]
+        for o in range(quarter):
+            got(OX[i * quarter + o])
+            kept = Y[me, piece(xh, o)].astype(F32) + RP[i * quarter + o].astype(F32)
+            OUT[piece(xh, o)] = kept.astype(BF16)
+            ref = OUT.at[piece(xh, o)]
+            last.append(send(ref, ref, core_peer))
+            store(piece(xh, o))
+    for i in range(2):
+        xh = (x, xo)[i]
+        for o in range(quarter):
+            got(last[i * quarter + o])
+            store(co * half + xh * quarter + o)
     for copy in stores:
         copy.wait()
     for copy in sent:
@@ -297,6 +309,8 @@
             pltpu.VMEM((n_planes, n_y, rows, width), BF16),
             pltpu.VMEM((n_planes, rows, width), BF16),
             pltpu.VMEM((n_planes - 1, quarter, rows, width), BF16),
+            pltpu.VMEM((half, rows, width), BF16),
+            pltpu.VMEM((half, rows, width), BF16),
             pltpu.VMEM((pieces, rows, width), BF16),
             pltpu.SemaphoreType.DMA((96,)),
             pltpu.SemaphoreType.DMA((96,)),

time: 113 us -> 109 us (0.965); the launches traced: 111 us -> 109 us
  Pallas kernels: 104 us -> 102 us
    pallas_call x1, Pallas kernels: 104 us -> 102 us  [planned(): pl.pallas_call(functools.partial(kernel, n_y, n_planes), name='moe', out_...]
where the time goes in v3:
time: 109 us
  Pallas kernels  102 us (94%)
  other arithmetic  3.38 us (3%)
  local copies, waits for them, and re-layouts  2.36 us (2%)
  between operations  1.3 us (1%)
    pallas_call x1, Pallas kernels, planned(): pl.pallas_call(functools.partial(kernel, n_y, n_planes), name='moe', out_...  102 us
    unnamed x1, local copies, waits for them, and re-layouts  2.29 us

profile of v3, /device:TPU:11, one launch (start us, length us, event | category | flops | bytes accessed | tf_op | source)
XLA Modules:
  0.0 108.7 jit_solution(5622984933959425305)
XLA Ops:
  1.3 0.7 fusion.3
  2.0 0.8 convert_reduce_fusion
  2.8 0.1 pad.5.clone
  2.9 0.7 fusion.meta
  3.6 101.6 %moe.1 = (bf16[128,4096]{1,0:T(8,128)(2,1)}, f32[8,128]{1,0:T(8,128)}) custom-call(bf16[128,4096]{1,0:T(8,128)(2,1)} %tokens.1, f32[8,128]{1,0:T(8,128)} %fusion.meta, bf16[1,4096,1024]{2,1,0:T(8,128)(2,1)} %w_gate.1, bf16[1,4096,1024]{2,1,0:T(8,128)(2,1)} %w_up.1, bf16[1,1024,4096]{2,1,0:T(8,128)(2,1)} %w_down.1), custom_call_target="tpu_custom_call" | custom-call | tf_op jit(solution)/shard_map/moe/pallas_call | solution.py:292
  105.2 1.2 %convert_bitcast_fusion = s32[4]{0:T(128)} fusion(f32[8,128]{1,0:T(8,128)} %get-tuple-element.17), kind=kLoop, calls=%fused_computation.10 | loop fusion | flops 4 | bytes 32 | tf_op jit(solution)/shard_map/convert_element_type | solution.py:323
  106.4 2.3 %copy.12 = bf16[128,4096]{1,0:T(8,128)(2,1)} copy(bf16[128,4096]{1,0:T(8,128)(2,1)} %get-tuple-element.20) | data formatting | bytes 2097152
  (3 shorter events, 0.0 us)
